TPU v7x, 128 devices: a whole 4x4x4 slice. The times are simulated.
128 devices in a mesh: samp: 4 (over z), row: 4 (over x_lo, core), col: 8 (over x_hi, y).
Axes of the slice: x: 4 (x_hi: 2, x_lo: 2; x = x_hi * 2 + x_lo), y: 4, z: 4, core: 2. Of those that a mesh axis runs over, the one named last changes fastest.
Arguments:
- pair: float32 [4, 320, 320, 128], P('samp', 'row', 'col'), may hold values from -6 to 6
- cotangent: float32 [4, 320, 320, 128], P('samp', 'row', 'col'), may hold values from -6 to 6
- crop_length: int32 [4], P('samp'), may hold values from 160 to 320
- in_gain: float32 [128], replicated, may hold values from 0.5 to 1.5
- in_bias: float32 [128], replicated, may hold values from -1.5 to 1.5
- proj_weight: bfloat16 [128, 512], replicated, may hold values from -0.5 to 0.5
- gate_weight: bfloat16 [128, 128], replicated, may hold values from -0.5 to 0.5
- out_gain: float32 [128], replicated, may hold values from 0.5 to 1.5
- out_bias: float32 [128], replicated, may hold values from -1.5 to 1.5
- out_weight: bfloat16 [128, 128], replicated, may hold values from -0.5 to 0.5
Outputs:
- grad_pair: float32 [4, 320, 320, 128], P('samp', 'row', 'col')
- grad_in_gain: float32 [128], replicated
- grad_in_bias: float32 [128], replicated
- grad_proj_weight: float32 [128, 512], replicated
- grad_gate_weight: float32 [128, 128], replicated
- grad_out_gain: float32 [128], replicated
- grad_out_bias: float32 [128], replicated
- grad_out_weight: float32 [128, 128], replicated
All inputs are finite; a program needn't handle non-finite values.
Results may differ from a plain program's by a relative error of at most 0.012.
Values may be sent and summed in bfloat16 or wider, within the bound.
No kernel may reach another device: no remote copies, remote signals or barrier semaphores. Data moves between devices by JAX's collectives and lax.ppermute only.
A program may use at most 128 MiB of HBM per device.

v0:
```python
import jax
import jax.numpy as jnp
from jax import lax
from jax.sharding import PartitionSpec as P

epsilon = 1e-05


def cut_along(shard, dim, length):
    before, after = (shard.shape[:dim], shard.shape[dim + 1 :])
    return jnp.moveaxis(shard.reshape(*before, length, -1, *after), dim, 0)


def piece_ends(length, count):
    unit = 8 if length >= 8 * count else 1
    return [length // unit * k // count * unit for k in range(1, count)]


def joined_along(parts, dim):
    parts = jnp.moveaxis(parts, 0, dim)
    lengths = parts.shape
    return parts.reshape(*lengths[:dim], lengths[dim] * lengths[dim + 1], *lengths[dim + 2 :])


def cut_exchange(shard, axis, pieces, split_dim, concat_dim):
    parts = cut_along(shard, split_dim, lax.axis_size(axis))
    widest = max(range(1, max(2, parts.ndim - 1)), key=lambda d: parts.shape[d])
    finished = []
    for share in jnp.split(parts, piece_ends(parts.shape[widest], pieces), axis=widest):
        if share.size:
            finished.append(lax.all_to_all(share, axis, split_axis=0, concat_axis=0, tiled=True))
    return joined_along(jnp.concatenate(finished, axis=widest), concat_dim)


def packed_total(arrays, axis):
    line, at, finished = (jnp.concatenate([a.reshape(-1) for a in arrays]), 0, [])
    subtotal = lax.psum(line, axis)
    for a in arrays:
        finished.append(subtotal[at : at + a.size].reshape(a.shape))
        at += a.size
    return tuple(finished)


def norm_stats(values):
    centre = jnp.mean(values, axis=-1, keepdims=True)
    centered = values - centre
    variance = jnp.mean(centered * centered, axis=-1, keepdims=True)
    inverse = lax.rsqrt(variance + epsilon)
    return (centered * inverse, inverse)


def norm_back(upstream, normal, inverse, weights):
    scaled = upstream * weights
    return inverse * (
        scaled
        - jnp.mean(scaled, axis=-1, keepdims=True)
        - normal * jnp.mean(scaled * normal, axis=-1, keepdims=True)
    )


def per_device(
    pair,
    cotangent,
    crop_length,
    in_gain,
    in_bias,
    proj_weight,
    gate_weight,
    out_gain,
    out_bias,
    out_weight,
):
    pair_tile = pair[0]
    upstream = cotangent[0]
    height, breadth, channels = pair_tile.shape
    hidden = out_weight.shape[0]
    row_first = lax.axis_index("row") * height
    col_first = lax.axis_index("col") * breadth
    crop_end = crop_length[0]
    row_live = (row_first + jnp.arange(height, dtype=jnp.int32) < crop_end).astype(jnp.float32)
    col_live = (col_first + jnp.arange(breadth, dtype=jnp.int32) < crop_end).astype(jnp.float32)
    live_mask = row_live[:, None, None] * col_live[None, :, None]
    in_hat, in_scale = norm_stats(pair_tile)
    normed = (in_hat * in_gain + in_bias).astype(jnp.bfloat16)
    flat_normed = normed.reshape(-1, channels)
    projected = jnp.dot(flat_normed, proj_weight, preferred_element_type=jnp.float32).reshape(
        height, breadth, 4 * hidden
    )
    left_sig = jax.nn.sigmoid(projected[..., :hidden])
    left_value = projected[..., hidden : 2 * hidden]
    right_sig = jax.nn.sigmoid(projected[..., 2 * hidden : 3 * hidden])
    right_value = projected[..., 3 * hidden :]
    left_factor = (left_sig * left_value * live_mask).astype(jnp.bfloat16)
    right_factor = (right_sig * right_value * live_mask).astype(jnp.bfloat16)
    right_rows = lax.all_gather(right_factor, "row", axis=0, tiled=True)
    right_turned = cut_exchange(right_rows, "col", 2, 0, 1)
    left_rows = lax.all_gather(left_factor, "col", axis=1, tiled=True)
    product = jnp.einsum(
        "ikh,jkh->ijh", left_rows, right_turned, preferred_element_type=jnp.float32
    )
    tri_hat, tri_scale = norm_stats(product)
    tri_normed = (tri_hat * out_gain + out_bias).astype(jnp.bfloat16)
    flat_tri = tri_normed.reshape(-1, hidden)
    out_value = jnp.dot(flat_tri, out_weight, preferred_element_type=jnp.float32)
    gate_value = jax.nn.sigmoid(
        jnp.dot(flat_normed, gate_weight, preferred_element_type=jnp.float32)
    )
    flat_up = upstream.reshape(-1, channels)
    d_out = (flat_up * gate_value).astype(jnp.bfloat16)
    d_gate = (flat_up * out_value * gate_value * (1.0 - gate_value)).astype(jnp.bfloat16)
    g_out_weight = jnp.dot(flat_tri.T, d_out, preferred_element_type=jnp.float32)
    d_tri_normed = jnp.dot(d_out, out_weight.T, preferred_element_type=jnp.float32).reshape(
        height, breadth, hidden
    )
    g_out_gain = jnp.sum(d_tri_normed * tri_hat, axis=(0, 1))
    g_out_bias = jnp.sum(d_tri_normed, axis=(0, 1))
    d_product = norm_back(d_tri_normed, tri_hat, tri_scale, out_gain).astype(jnp.bfloat16)
    grad_full = lax.all_gather(d_product, "col", axis=1, tiled=True)
    d_left = jnp.einsum("ijh,jkh->ikh", grad_full, right_rows, preferred_element_type=jnp.float32)
    d_right = lax.psum_scatter(
        jnp.einsum(
            "ijh,ikh->jkh", grad_full, left_factor, preferred_element_type=jnp.float32
        ).astype(jnp.bfloat16),
        "row",
        scatter_dimension=0,
        tiled=True,
    ).astype(jnp.float32)
    d_proj = (
        jnp.concatenate(
            [
                d_left * live_mask * left_value * left_sig * (1.0 - left_sig),
                d_left * live_mask * left_sig,
                d_right * live_mask * right_value * right_sig * (1.0 - right_sig),
                d_right * live_mask * right_sig,
            ],
            axis=-1,
        )
        .astype(jnp.bfloat16)
        .reshape(-1, 4 * hidden)
    )
    g_proj_weight = jnp.dot(flat_normed.T, d_proj, preferred_element_type=jnp.float32)
    g_gate_weight = jnp.dot(flat_normed.T, d_gate, preferred_element_type=jnp.float32)
    d_normed = (
        jnp.dot(d_proj, proj_weight.T, preferred_element_type=jnp.float32)
        + jnp.dot(d_gate, gate_weight.T, preferred_element_type=jnp.float32)
    ).reshape(height, breadth, channels)
    g_in_gain = jnp.sum(d_normed * in_hat, axis=(0, 1))
    g_in_bias = jnp.sum(d_normed, axis=(0, 1))
    grad_pair = norm_back(d_normed, in_hat, in_scale, in_gain)
    totals = packed_total(
        (g_in_gain, g_in_bias, g_proj_weight, g_gate_weight, g_out_gain, g_out_bias, g_out_weight),
        ("samp", "row", "col"),
    )
    factor = 1.0 / (breadth * lax.axis_size("col"))
    return (
        grad_pair[None],
        totals[0] * factor,
        totals[1] * factor,
        totals[2] * factor,
        totals[3] * factor,
        totals[4] * factor,
        totals[5] * factor,
        totals[6] * factor,
    )


def solution(mesh):
    return jax.shard_map(
        per_device,
        mesh=mesh,
        in_specs=(
            P("samp", "row", "col", None),
            P("samp", "row", "col", None),
            P("samp"),
            P(),
            P(),
            P(),
            P(),
            P(),
            P(),
            P(),
        ),
        out_specs=(P("samp", "row", "col", None), P(), P(), P(), P(), P(), P(), P()),
        check_vma=False,
    )
```

profile of v0, /device:TPU:1, one launch (start us, length us, event | category | flops | bytes accessed | tf_op | source)
XLA Modules:
  0.0 551.7 jit_solution(769624488051377025)
XLA Ops:
  7.3 2.0 reduce_sum.108
  12.4 2.5 multiply_convert_fusion.5
  16.4 42.1 %all-gather.4.cloned.1.call-done = bf16[320,40,128]{2,1,0:T(8,128)(2,1)} async-done(((bf16[80,40,128]{2,1,0:T(8,128)(2,1)}), bf16[320,40,128]{2,1,0:T(8,128)(2,1)}) %all-gather.4.cloned.1.call-update) | async-done | bytes 3276816 | tf_op jit(solution)/shard_map/all_gather | solution.py:95
  58.5 2.5 split.8
  61.0 6.1 %all-to-all-start = ((bf16[8,16,40,128]{3,2,1,0:T(8,128)(2,1)}), bf16[8,16,40,128]{3,2,1,0:T(8,128)(2,1)S(1)}, u32[]{:S(2)}, u32[]{:S(2)}) async-start(bf16[8,16,40,128]{3,2,1,0:T(8,128)(2,1)} %split.8), calls=%async_computation | async-start | bytes 2621440 | tf_op jit(solution)/shard_map/all_to_all | solution.py:31
  67.4 3.2 split.9
  70.6 23.4 %all-to-all-done = bf16[8,16,40,128]{3,2,1,0:T(8,128)(2,1)S(1)} async-done(((bf16[8,16,40,128]{3,2,1,0:T(8,128)(2,1)}), bf16[8,16,40,128]{3,2,1,0:T(8,128)(2,1)S(1)}, u32[]{:S(2)}, u32[]{:S(2)}) %all-to-all-start) | async-done | bytes 1310752 | tf_op jit(solution)/shard_map/all_to_all | solution.py:31
  94.0 4.3 all-to-all-start.1
  100.4 1.8 fusion.29
  104.2 2.1 copy.73
  106.5 19.8 %all-to-all-done.1 = bf16[8,24,40,128]{3,2,1,0:T(8,128)(2,1)} async-done(((bf16[8,24,40,128]{3,2,1,0:T(8,128)(2,1)}), bf16[8,24,40,128]{3,2,1,0:T(8,128)(2,1)}, u32[]{:S(2)}, u32[]{:S(2)}) %all-to-all-start.1) | async-done | bytes 1966112 | tf_op jit(solution)/shard_map/all_to_all | solution.py:31
  126.3 1.8 pad_maximum_fusion
  129.1 4.4 copy.67
  133.5 38.1 %all-gather.6.cloned.1.call-done = bf16[80,320,128]{2,1,0:T(8,128)(2,1)} async-done(((bf16[80,40,128]{2,1,0:T(8,128)(2,1)}), bf16[80,320,128]{2,1,0:T(8,128)(2,1)}) %all-gather.6.cloned.1.call-update) | async-done | bytes 6553616 | tf_op jit(solution)/shard_map/all_gather | solution.py:97
  171.6 14.4 %copy.68 = bf16[80,320,128]{0,1,2:T(8,128)(2,1)} copy(bf16[80,320,128]{2,1,0:T(8,128)(2,1)} %all-gather.6.cloned.1.call-done) | data formatting | bytes 13107200 | tf_op jit(solution)/shard_map/all_gather | solution.py:97
  186.0 7.3 %bitcast_reduce_fusion = (f32[80,40]{0,1:T(8,128)S(1)}, f32[128,40,80]{2,1,0:T(8,128)S(1)}) fusion(bf16[40,320,128]{1,0,2:T(8,128)(2,1)} %copy.67, bf16[80,320,128]{0,1,2:T(8,128)(2,1)} %copy.68), kind=kOutput, calls=%fused_computation.27 | convolution fusion | flops 262550400 | bytes 11481600 | tf_op jit(solution)/shard_map/ikh,jkh->ijh/dot_general | solution.py:98
  194.1 3.6 multiply_reduce_fusion
  197.9 4.3 multiply_convert_fusion
  204.8 119.7 %all-gather.8.cloned.1.call-done = bf16[80,320,128]{0,1,2:T(8,128)(2,1)} async-done(((bf16[80,40,128]{0,1,2:T(8,128)(2,1)}), bf16[80,320,128]{0,1,2:T(8,128)(2,1)}) %all-gather.8.cloned.1.call-update) | async-done | bytes 6553616 | tf_op jit(solution)/shard_map/all_gather | solution.py:118
  324.5 9.2 %fusion.41 = bf16[128,40,320]{2,1,0:T(8,128)(2,1)} fusion(bf16[80,40,128]{0,1,2:T(8,128)(2,1)S(1)} %copy.79, bf16[80,320,128]{0,1,2:T(8,128)(2,1)} %all-gather.8.cloned.1.call-done), kind=kOutput, calls=%fused_computation.99 | convolution fusion | flops 262144000 | bytes 10649600 | tf_op jit(solution)/shard_map/ijh,ikh->jkh/dot_general | solution.py:121
  333.7 6.7 %copy.80 = bf16[128,40,320]{0,1,2:T(8,128)(2,1)} copy(bf16[128,40,320]{2,1,0:T(8,128)(2,1)} %fusion.41) | data formatting | bytes 6553600 | tf_op jit(solution)/shard_map/ijh,ikh->jkh/dot_general | solution.py:121
  340.4 1.8 copy-done.5
  342.3 4.9 copy.77
  347.2 2.8 copy.81
  351.1 1.9 fusion.5
  355.7 5.4 fusion.40
  361.1 2.0 copy.78
  363.1 14.1 %reduce-scatter.2.cloned.1.call-done = bf16[80,40,128]{2,1,0:T(8,128)(2,1)} async-done(((bf16[320,40,128]{2,1,0:T(8,128)(2,1)}), bf16[80,40,128]{2,1,0:T(8,128)(2,1)}) %reduce-scatter.2.cloned.1.call-update) | async-done | bytes 819216 | tf_op jit(solution)/shard_map/reduce_scatter | solution.py:120
  377.2 4.4 multiply_convert_fusion.4
  383.5 2.0 multiply_reduce_fusion.3
  397.5 4.1 subtract_multiply_fusion
  401.6 138.9 %all-reduce.2.cloned.1.call-done = f32[98816]{0:T(1024)} async-done(((f32[98816]{0:T(1024)}), f32[98816]{0:T(1024)}) %all-reduce.2.cloned.1.call-update) | async-done | bytes 395280 | tf_op jit(solution)/shard_map/psum | solution.py:37
  (119 shorter events, 34.7 us)
Async XLA Ops:
  7.2 3.9 copy-start
  7.2 2.1 copy-start.2
  7.2 51.4 %all-gather.4.cloned.1.call-start = ((), (), s32[]{:S(2)}) async-start(), calls=%async_computation.3 | async-start | bytes 4096000 | tf_op jit(solution)/shard_map/all_gather | solution.py:95
  7.2 3.8 copy-start.25
  7.3 3.8 copy-start.27
  12.4 3.3 copy-start.1
  15.7 155.9 %all-gather.6.cloned.1.call-start = ((), (), s32[]{:S(2)}) async-start(), calls=%async_computation.4 | async-start | bytes 7372800 | tf_op jit(solution)/shard_map/all_gather | solution.py:97
  61.0 32.9 %all-to-all-start = ((bf16[8,16,40,128]{3,2,1,0:T(8,128)(2,1)}), bf16[8,16,40,128]{3,2,1,0:T(8,128)(2,1)S(1)}, u32[]{:S(2)}, u32[]{:S(2)}) async-start(bf16[8,16,40,128]{3,2,1,0:T(8,128)(2,1)} %split.8), calls=%async_computation | async-start | bytes 2621440 | tf_op jit(solution)/shard_map/all_to_all | solution.py:31
  67.3 31.3 %copy-start.18 = (f32[3200]{0:T(1024)}, f32[3200]{0:T(1024)S(1)}, u32[]{:S(2)}) copy-start(f32[3200]{0:T(1024)S(1)} %rsqrt.22) | copy-start | bytes 38404
  67.4 31.2 %copy-start.20 = (f32[3200]{0:T(1024)}, f32[3200]{0:T(1024)S(1)}, u32[]{:S(2)}) copy-start(f32[3200]{0:T(1024)S(1)} %div.47) | copy-start | bytes 38404
  94.0 32.4 %all-to-all-start.1 = ((bf16[8,24,40,128]{3,2,1,0:T(8,128)(2,1)}), bf16[8,24,40,128]{3,2,1,0:T(8,128)(2,1)}, u32[]{:S(2)}, u32[]{:S(2)}) async-start(bf16[8,24,40,128]{3,2,1,0:T(8,128)(2,1)} %split.9), calls=%async_computation.1 | async-start | bytes 3932160 | tf_op jit(solution)/shard_map/all_to_all | solution.py:31
  98.3 2.0 copy-start.22
  98.3 226.1 %all-gather.8.cloned.1.call-start = ((), (), s32[]{:S(2)}) async-start(), calls=%async_computation.5 | async-start | bytes 11796480 | tf_op jit(solution)/shard_map/all_gather | solution.py:118
  100.4 1.8 copy-start.7
  100.4 2.7 copy-start.16
  100.4 2.7 copy-start.24
  194.1 3.8 copy-start.29
  202.2 175.0 %reduce-scatter.2.cloned.1.call-start = ((), (), s32[]{:S(2)}) async-start(), calls=%async_computation.6 | async-start | bytes 4096000 | tf_op jit(solution)/shard_map/reduce_scatter | solution.py:120
  340.4 1.9 copy-start.5
  340.4 200.2 %all-reduce.2.cloned.1.call-start = ((), (), s32[]{:S(2)}) async-start(), calls=%async_computation.7 | async-start | bytes 794624 | tf_op jit(solution)/shard_map/psum | solution.py:37
  347.2 2.9 copy-start.10
  347.2 3.9 copy-start.12
  351.1 2.0 copy-start.8
  351.1 3.0 copy-start.23
  353.1 2.6 copy-start.4
  363.1 18.5 %copy-start.3 = (f32[1,80,40,128]{3,2,1,0:T(8,128)S(1)}, f32[1,80,40,128]{3,2,1,0:T(8,128)}, u32[]{:S(2)}) copy-start(f32[1,80,40,128]{3,2,1,0:T(8,128)} %param.10) | copy-start | bytes 4915204
  363.1 18.5 %copy-start.26 = (f32[128]{0:T(128)S(1)}, f32[128]{0:T(128)}, u32[]{:S(2)}) copy-start(f32[128]{0:T(128)} %param.13) | copy-start | bytes 1540
  363.1 18.5 %copy-start.28 = (f32[128]{0:T(128)S(1)}, f32[128]{0:T(128)}, u32[]{:S(2)}) copy-start(f32[128]{0:T(128)} %param.14) | copy-start | bytes 1540
  383.4 6.3 %copy-start.15 = (f32[16384]{0:T(1024)S(1)}, f32[16384]{0:T(1024)}, u32[]{:S(2)}) copy-start(f32[16384]{0:T(1024)} %convolution_bitcast_fusion.1) | copy-start | bytes 196612
  383.4 7.8 %copy-start.31 = (f32[128]{0:T(128)S(1)}, f32[128]{0:T(128)}, u32[]{:S(2)}) copy-start(f32[128]{0:T(128)} %get-tuple-element.8) | copy-start | bytes 1540
  383.5 9.1 %copy-start.30 = (f32[128]{0:T(128)S(1)}, f32[128]{0:T(128)}, u32[]{:S(2)}) copy-start(f32[128]{0:T(128)} %get-tuple-element.13) | copy-start | bytes 1540
  383.5 10.4 %copy-start.14 = (f32[16384]{0:T(1024)S(1)}, f32[16384]{0:T(1024)}, u32[]{:S(2)}) copy-start(f32[16384]{0:T(1024)} %convolution_bitcast_fusion) | copy-start | bytes 196612
  (7 other events, 10.1 us)
Sparse Core Ops, SparseCore 0:
  15.8 42.7 all-gather.3
  61.0 110.5 all-gather.5
  202.4 122.0 all-gather.7
  340.5 36.6 reduce-scatter.1
  395.5 144.9 all-reduce.1
where the time goes:
time: 553 us; the launch traced here: 552 us
  waiting for transfers between devices  397 us (72%)
  local copies, waits for them, and re-layouts  62.9 us (11%)
  matrix products  35.3 us (6%)
  other arithmetic  30.6 us (6%)
  between operations  15 us (3%)
  starting transfers between devices  11.1 us (2%)
    psum x1, waiting for transfers between devices, packed_total(): subtotal = lax.psum(line, axis)  139 us
    all_gather x1, waiting for transfers between devices, per_device(): grad_full = lax.all_gather(d_product, 'col', axis=1, tiled=True)  120 us
    all_to_all x2, waiting for transfers between devices, cut_exchange(): lax.all_to_all(share, axis, split_axis=0, concat_axis=0, tiled=True)  43.2 us
    all_gather x1, waiting for transfers between devices, per_device(): right_rows = lax.all_gather(right_factor, 'row', axis=0, tiled=True)  42.1 us
    all_gather x1, waiting for transfers between devices, per_device(): left_rows = lax.all_gather(left_factor, 'col', axis=1, tiled=True)  38.1 us
    all_gather x1, local copies, waits for them, and re-layouts, per_device(): left_rows = lax.all_gather(left_factor, 'col', axis=1, tiled=True)  14.4 us
    reduce_scatter x1, waiting for transfers between devices, per_device(): lax.psum_scatter(jnp.einsum('ijh,ikh->jkh', grad_full, left_factor, prefe...  14.1 us
    unnamed x71, local copies, waits for them, and re-layouts  12.9 us
  transfers between devices with their start and end apart: 7, of which 7 were waited for; matrix products, arithmetic and copies ran while one was open for 9% of the time, Pallas kernels for 0%

commit v1 on v0

--- a/solution.py
+++ b/solution.py
@@ -115,7 +115,9 @@
     g_out_gain = jnp.sum(d_tri_normed * tri_hat, axis=(0, 1))
     g_out_bias = jnp.sum(d_tri_normed, axis=(0, 1))
     d_product = norm_back(d_tri_normed, tri_hat, tri_scale, out_gain).astype(jnp.bfloat16)
-    grad_full = lax.all_gather(d_product, "col", axis=1, tiled=True)
+    grad_full = jnp.concatenate(
+        lax.all_to_all(jnp.stack([d_product] * lax.axis_size("col")), "col", 0, 0), axis=1
+    )
     d_left = jnp.einsum("ijh,jkh->ikh", grad_full, right_rows, preferred_element_type=jnp.float32)
     d_right = lax.psum_scatter(
         jnp.einsum(

time: 553 us -> 533 us (0.964)
  waiting for transfers between devices: 397 us -> 351 us
  local copies, waits for them, and re-layouts: 62.9 us -> 85.9 us
    all_gather x1 -> x0, waiting for transfers between devices: 120 us -> none  [per_device(): grad_full = lax.all_gather(d_product, 'col', axis=1, tiled=True)]
    all_to_all x0 -> x1, waiting for transfers between devices: none -> 72.3 us  [per_device(): lax.all_to_all(jnp.stack([d_product] * lax.axis_size('col')), 'col', 0, 0)]
    reshape x0 -> x1, local copies, waits for them, and re-layouts: none -> 10.7 us  [per_device(): jnp.concatenate(lax.all_to_all(jnp.stack([d_product] * lax.axis_size('col...]
    all_to_all x0 -> x1, local copies, waits for them, and re-layouts: none -> 7.48 us  [per_device(): lax.all_to_all(jnp.stack([d_product] * lax.axis_size('col')), 'col', 0, 0)]
where the time goes in v1:
time: 533 us; the launch traced here: 531 us
  waiting for transfers between devices  351 us (66%)
  local copies, waits for them, and re-layouts  85.9 us (16%)
  matrix products  32.4 us (6%)
  other arithmetic  30.6 us (6%)
  starting transfers between devices  15.9 us (3%)
  between operations  15 us (3%)
    psum x1, waiting for transfers between devices, packed_total(): subtotal = lax.psum(line, axis)  139 us
    all_to_all x1, waiting for transfers between devices, per_device(): lax.all_to_all(jnp.stack([d_product] * lax.axis_size('col')), 'col', 0, 0)  72.3 us
    all_to_all x2, waiting for transfers between devices, cut_exchange(): lax.all_to_all(share, axis, split_axis=0, concat_axis=0, tiled=True)  43.4 us
    all_gather x1, waiting for transfers between devices, per_device(): right_rows = lax.all_gather(right_factor, 'row', axis=0, tiled=True)  42.1 us
    all_gather x1, waiting for transfers between devices, per_device(): left_rows = lax.all_gather(left_factor, 'col', axis=1, tiled=True)  38 us
    reduce_scatter x1, waiting for transfers between devices, per_device(): lax.psum_scatter(jnp.einsum('ijh,ikh->jkh', grad_full, left_factor, prefe...  15.8 us
    all_gather x1, local copies, waits for them, and re-layouts, per_device(): left_rows = lax.all_gather(left_factor, 'col', axis=1, tiled=True)  14.4 us
    unnamed x71, local copies, waits for them, and re-layouts  12.1 us
  transfers between devices with their start and end apart: 7, of which 7 were waited for; matrix products, arithmetic and copies ran while one was open for 9% of the time, Pallas kernels for 0%

profile of v1, /device:TPU:1, one launch (start us, length us, event | category | flops | bytes accessed | tf_op | source)
XLA Modules:
  0.0 531.0 jit_solution(16127647783181152139)
XLA Ops:
  7.3 2.0 reduce_sum.108
  12.4 2.6 multiply_convert_fusion.5
  16.4 42.1 %all-gather.3.cloned.1.call-done = bf16[320,40,128]{2,1,0:T(8,128)(2,1)} async-done(((bf16[80,40,128]{2,1,0:T(8,128)(2,1)}), bf16[320,40,128]{2,1,0:T(8,128)(2,1)}) %all-gather.3.cloned.1.call-update) | async-done | bytes 3276816 | tf_op jit(solution)/shard_map/all_gather | solution.py:95
  58.5 2.5 split.8
  61.0 6.1 %all-to-all-start = ((bf16[8,16,40,128]{3,2,1,0:T(8,128)(2,1)}), bf16[8,16,40,128]{3,2,1,0:T(8,128)(2,1)S(1)}, u32[]{:S(2)}, u32[]{:S(2)}) async-start(bf16[8,16,40,128]{3,2,1,0:T(8,128)(2,1)} %split.8), calls=%async_computation | async-start | bytes 2621440 | tf_op jit(solution)/shard_map/all_to_all | solution.py:31
  67.4 3.2 split.9
  70.6 23.4 %all-to-all-done = bf16[8,16,40,128]{3,2,1,0:T(8,128)(2,1)S(1)} async-done(((bf16[8,16,40,128]{3,2,1,0:T(8,128)(2,1)}), bf16[8,16,40,128]{3,2,1,0:T(8,128)(2,1)S(1)}, u32[]{:S(2)}, u32[]{:S(2)}) %all-to-all-start) | async-done | bytes 1310752 | tf_op jit(solution)/shard_map/all_to_all | solution.py:31
  94.0 4.5 all-to-all-start.1
  104.1 2.1 copy.81
  106.4 20.0 %all-to-all-done.1 = bf16[8,24,40,128]{3,2,1,0:T(8,128)(2,1)} async-done(((bf16[8,24,40,128]{3,2,1,0:T(8,128)(2,1)}), bf16[8,24,40,128]{3,2,1,0:T(8,128)(2,1)}, u32[]{:S(2)}, u32[]{:S(2)}) %all-to-all-start.1) | async-done | bytes 1966112 | tf_op jit(solution)/shard_map/all_to_all | solution.py:31
  129.2 4.3 copy.75
  133.5 38.0 %all-gather.5.cloned.1.call-done = bf16[80,320,128]{2,1,0:T(8,128)(2,1)} async-done(((bf16[80,40,128]{2,1,0:T(8,128)(2,1)}), bf16[80,320,128]{2,1,0:T(8,128)(2,1)}) %all-gather.5.cloned.1.call-update) | async-done | bytes 6553616 | tf_op jit(solution)/shard_map/all_gather | solution.py:97
  171.6 14.4 %copy.76 = bf16[80,320,128]{0,1,2:T(8,128)(2,1)} copy(bf16[80,320,128]{2,1,0:T(8,128)(2,1)} %all-gather.5.cloned.1.call-done) | data formatting | bytes 13107200 | tf_op jit(solution)/shard_map/all_gather | solution.py:97
  186.0 7.3 %bitcast_reduce_fusion = (f32[80,40]{0,1:T(8,128)S(1)}, f32[128,40,80]{2,1,0:T(8,128)S(1)}) fusion(bf16[40,320,128]{1,0,2:T(8,128)(2,1)} %copy.75, bf16[80,320,128]{0,1,2:T(8,128)(2,1)} %copy.76), kind=kOutput, calls=%fused_computation.27 | convolution fusion | flops 262550400 | bytes 11481600 | tf_op jit(solution)/shard_map/ikh,jkh->ijh/dot_general | solution.py:98
  194.1 3.6 multiply_reduce_fusion
  197.8 4.4 multiply_convert_fusion
  202.2 2.5 copy.85
  204.7 3.6 stack.2
  208.3 4.9 all-to-all-start.2
  214.9 72.3 %all-to-all-done.2 = bf16[8,80,40,128]{3,2,1,0:T(8,128)(2,1)} async-done(((bf16[8,80,40,128]{3,2,1,0:T(8,128)(2,1)}), bf16[8,80,40,128]{3,2,1,0:T(8,128)(2,1)}, u32[]{:S(2)}, u32[]{:S(2)}) %all-to-all-start.2) | async-done | bytes 6553632 | tf_op jit(solution)/shard_map/all_to_all | solution.py:119
  287.1 7.5 %copy.86 = bf16[8,80,40,128]{3,2,0,1:T(8,128)(2,1)} copy(bf16[8,80,40,128]{3,2,1,0:T(8,128)(2,1)} %all-to-all-done.2) | data formatting | bytes 13107200 | tf_op jit(solution)/shard_map/all_to_all | solution.py:119
  294.6 10.7 %copy.88 = bf16[80,320,128]{1,0,2:T(8,128)(2,1)} copy(bf16[80,320,128]{2,1,0:T(8,128)(2,1)} %bitcast.97) | data formatting | bytes 13107200 | tf_op jit(solution)/shard_map/reshape | solution.py:118
  305.3 6.6 %fusion.41 = bf16[128,40,320]{2,1,0:T(8,128)(2,1)} fusion(bf16[80,40,128]{0,1,2:T(8,128)(2,1)S(1)} %copy.90, bf16[80,320,128]{1,0,2:T(8,128)(2,1)} %copy.88), kind=kOutput, calls=%fused_computation.99 | convolution fusion | flops 262144000 | bytes 10649600 | tf_op jit(solution)/shard_map/ijh,ikh->jkh/dot_general | solution.py:123
  311.9 6.6 %copy.92 = bf16[128,40,320]{0,1,2:T(8,128)(2,1)} copy(bf16[128,40,320]{2,1,0:T(8,128)(2,1)} %fusion.41) | data formatting | bytes 6553600 | tf_op jit(solution)/shard_map/ijh,ikh->jkh/dot_general | solution.py:123
  320.5 4.9 copy.87
  325.4 2.6 copy.93
  333.6 5.1 fusion.40
  338.7 2.0 copy.89
  340.8 15.8 %reduce-scatter.2.cloned.1.call-done = bf16[80,40,128]{2,1,0:T(8,128)(2,1)} async-done(((bf16[320,40,128]{2,1,0:T(8,128)(2,1)}), bf16[80,40,128]{2,1,0:T(8,128)(2,1)}) %reduce-scatter.2.cloned.1.call-update) | async-done | bytes 819216 | tf_op jit(solution)/shard_map/reduce_scatter | solution.py:122
  356.6 4.4 multiply_convert_fusion.4
  376.9 4.1 subtract_multiply_fusion
  381.0 138.9 %all-reduce.2.cloned.1.call-done = f32[98816]{0:T(1024)} async-done(((f32[98816]{0:T(1024)}), f32[98816]{0:T(1024)}) %all-reduce.2.cloned.1.call-update) | async-done | bytes 395280 | tf_op jit(solution)/shard_map/psum | solution.py:37
  (122 shorter events, 42.9 us)
Async XLA Ops:
  7.2 3.9 copy-start
  7.2 2.1 copy-start.2
  7.2 51.3 %all-gather.3.cloned.1.call-start = ((), (), s32[]{:S(2)}) async-start(), calls=%async_computation.4 | async-start | bytes 4096000 | tf_op jit(solution)/shard_map/all_gather | solution.py:95
  7.2 3.8 copy-start.25
  7.3 3.8 copy-start.27
  12.4 3.3 copy-start.1
  15.7 155.9 %all-gather.5.cloned.1.call-start = ((), (), s32[]{:S(2)}) async-start(), calls=%async_computation.5 | async-start | bytes 7372800 | tf_op jit(solution)/shard_map/all_gather | solution.py:97
  61.0 32.9 %all-to-all-start = ((bf16[8,16,40,128]{3,2,1,0:T(8,128)(2,1)}), bf16[8,16,40,128]{3,2,1,0:T(8,128)(2,1)S(1)}, u32[]{:S(2)}, u32[]{:S(2)}) async-start(bf16[8,16,40,128]{3,2,1,0:T(8,128)(2,1)} %split.8), calls=%async_computation | async-start | bytes 2621440 | tf_op jit(solution)/shard_map/all_to_all | solution.py:31
  67.3 31.2 %copy-start.18 = (f32[3200]{0:T(1024)}, f32[3200]{0:T(1024)S(1)}, u32[]{:S(2)}) copy-start(f32[3200]{0:T(1024)S(1)} %rsqrt.22) | copy-start | bytes 38404
  67.4 31.1 %copy-start.20 = (f32[3200]{0:T(1024)}, f32[3200]{0:T(1024)S(1)}, u32[]{:S(2)}) copy-start(f32[3200]{0:T(1024)S(1)} %div.47) | copy-start | bytes 38404
  94.0 32.5 %all-to-all-start.1 = ((bf16[8,24,40,128]{3,2,1,0:T(8,128)(2,1)}), bf16[8,24,40,128]{3,2,1,0:T(8,128)(2,1)}, u32[]{:S(2)}, u32[]{:S(2)}) async-start(bf16[8,24,40,128]{3,2,1,0:T(8,128)(2,1)} %split.9), calls=%async_computation.1 | async-start | bytes 3932160 | tf_op jit(solution)/shard_map/all_to_all | solution.py:31
  100.3 1.8 copy-start.7
  100.3 2.7 copy-start.16
  100.3 2.7 copy-start.24
  194.1 3.8 copy-start.29
  208.3 5.2 copy-start.6
  208.3 78.8 %all-to-all-start.2 = ((bf16[8,80,40,128]{3,2,1,0:T(8,128)(2,1)}), bf16[8,80,40,128]{3,2,1,0:T(8,128)(2,1)}, u32[]{:S(2)}, u32[]{:S(2)}) async-start(bf16[8,80,40,128]{3,2,1,0:T(8,128)(2,1)} %stack.2), calls=%async_computation.2 | async-start | bytes 13107200 | tf_op jit(solution)/shard_map/all_to_all | solution.py:119
  213.2 143.4 %reduce-scatter.2.cloned.1.call-start = ((), (), s32[]{:S(2)}) async-start(), calls=%async_computation.6 | async-start | bytes 4096000 | tf_op jit(solution)/shard_map/reduce_scatter | solution.py:122
  318.6 1.9 copy-start.5
  318.6 201.3 %all-reduce.2.cloned.1.call-start = ((), (), s32[]{:S(2)}) async-start(), calls=%async_computation.7 | async-start | bytes 794624 | tf_op jit(solution)/shard_map/psum | solution.py:37
  325.4 2.6 copy-start.10
  325.4 3.7 copy-start.12
  329.1 1.9 copy-start.8
  329.1 3.0 copy-start.23
  331.0 2.6 copy-start.4
  340.8 20.2 %copy-start.3 = (f32[1,80,40,128]{3,2,1,0:T(8,128)S(1)}, f32[1,80,40,128]{3,2,1,0:T(8,128)}, u32[]{:S(2)}) copy-start(f32[1,80,40,128]{3,2,1,0:T(8,128)} %param.10) | copy-start | bytes 4915204
  340.8 20.2 %copy-start.26 = (f32[128]{0:T(128)S(1)}, f32[128]{0:T(128)}, u32[]{:S(2)}) copy-start(f32[128]{0:T(128)} %param.13) | copy-start | bytes 1540
  340.8 20.2 %copy-start.28 = (f32[128]{0:T(128)S(1)}, f32[128]{0:T(128)}, u32[]{:S(2)}) copy-start(f32[128]{0:T(128)} %param.14) | copy-start | bytes 1540
  362.8 6.3 %copy-start.15 = (f32[16384]{0:T(1024)S(1)}, f32[16384]{0:T(1024)}, u32[]{:S(2)}) copy-start(f32[16384]{0:T(1024)} %convolution_bitcast_fusion.1) | copy-start | bytes 196612
  362.8 7.8 %copy-start.31 = (f32[128]{0:T(128)S(1)}, f32[128]{0:T(128)}, u32[]{:S(2)}) copy-start(f32[128]{0:T(128)} %get-tuple-element.8) | copy-start | bytes 1540
  362.8 9.1 %copy-start.30 = (f32[128]{0:T(128)S(1)}, f32[128]{0:T(128)}, u32[]{:S(2)}) copy-start(f32[128]{0:T(128)} %get-tuple-element.13) | copy-start | bytes 1540
  362.8 10.4 %copy-start.14 = (f32[16384]{0:T(1024)S(1)}, f32[16384]{0:T(1024)}, u32[]{:S(2)}) copy-start(f32[16384]{0:T(1024)} %convolution_bitcast_fusion) | copy-start | bytes 196612
  (7 other events, 10.7 us)
Sparse Core Ops, SparseCore 0:
  15.8 42.7 all-gather.2
  60.9 110.5 all-gather.4
  318.7 37.8 reduce-scatter.1
  374.9 144.9 all-reduce.1
